TPU v7x, 32 devices: a whole 2x2x4 slice. The times are simulated.
32 devices in a mesh: dp: 8 (over y, x, core), seq: 4 (over z).
Axes of the slice: x: 2, y: 2, z: 4, core: 2. Of those that a mesh axis runs over, the one named last changes fastest.
Arguments:
- layer_input: bfloat16 [8, 512, 2048], P('dp', 'seq'), may hold values from -6 to 6
- cotangent: bfloat16 [8, 512, 2048], P('dp', 'seq'), may hold values from -6 to 6
- ln1_gain: float32 [2048], P('dp'), may hold values from 0.5 to 1.5
- ln1_bias: float32 [2048], P('dp'), may hold values from -3 to 3
- w_qkv: bfloat16 [2048, 6144], P('dp'), may hold values from -0.125 to 0.125
- b_qkv: float32 [6144], P('dp'), may hold values from -3 to 3
- w_out: bfloat16 [2048, 2048], P('dp'), may hold values from -0.5 to 0.5
- b_out: float32 [2048], P('dp'), may hold values from -3 to 3
- ln2_gain: float32 [2048], P('dp'), may hold values from 0.5 to 1.5
- ln2_bias: float32 [2048], P('dp'), may hold values from -3 to 3
- w_up: bfloat16 [2048, 8192], P('dp'), may hold values from -0.125 to 0.125
- b_up: float32 [8192], P('dp'), may hold values from -3 to 3
- w_down: bfloat16 [8192, 2048], P('dp'), may hold values from -0.0625 to 0.0625
- b_down: float32 [2048], P('dp'), may hold values from -3 to 3
Outputs:
- output: float32 [8, 512, 2048], P('dp', 'seq')
- input_grad: float32 [8, 512, 2048], P('dp', 'seq')
- ln1_gain_grad: float32 [2048], P('dp')
- ln1_bias_grad: float32 [2048], P('dp')
- w_qkv_grad: float32 [2048, 6144], P('dp')
- b_qkv_grad: float32 [6144], P('dp')
- w_out_grad: float32 [2048, 2048], P('dp')
- b_out_grad: float32 [2048], P('dp')
- ln2_gain_grad: float32 [2048], P('dp')
- ln2_bias_grad: float32 [2048], P('dp')
- w_up_grad: float32 [2048, 8192], P('dp')
- b_up_grad: float32 [8192], P('dp')
- w_down_grad: float32 [8192, 2048], P('dp')
- b_down_grad: float32 [2048], P('dp')
All inputs are finite; a program needn't handle non-finite values.
Results may differ from a plain program's by a relative error of at most 0.029.
Values may be sent and summed in bfloat16 or wider, within the bound.
A program may use at most 640 MiB of HBM per device.

v0:
```python
import jax
import jax.numpy as jnp
from jax import lax
from jax.sharding import PartitionSpec as P

H = 8
HD = 256
ROT = 64
epsilon = 1e-05
masked_fill = -1e30


def normalize(rows, gain, shift):
    center = rows - jnp.mean(rows, axis=-1, keepdims=True)
    factor = lax.rsqrt(jnp.mean(center * center, axis=-1, keepdims=True) + epsilon)
    normed = center * factor
    return (normed, factor, normed * gain + shift)


def normalize_back(incoming, normed, factor, gain):
    scaled = incoming * gain
    return factor * (
        scaled
        - jnp.mean(scaled, axis=-1, keepdims=True)
        - normed * jnp.mean(scaled * normed, axis=-1, keepdims=True)
    )


def gelu_value(inner):
    return inner * 0.5 * (1.0 + jax.scipy.special.erf(inner * 0.7071067811865476))


def gelu_slope(inner):
    cumulative = 0.5 * (1.0 + jax.scipy.special.erf(inner * 0.7071067811865476))
    return cumulative + inner * jnp.exp(-0.5 * inner * inner) * 0.3989422804014327


def angles(positions):
    half = ROT // 2
    freqs = 10000.0 ** (-2.0 * jnp.arange(half).astype(positions.dtype) / ROT)
    theta = positions[:, None] * freqs[None, :]
    return (jnp.cos(theta), jnp.sin(theta))


def rotate(tensor, cosine, sine, direction):
    half = ROT // 2
    first_half = tensor[..., :half]
    second_half = tensor[..., half:ROT]
    return jnp.concatenate(
        [
            first_half * cosine - direction * second_half * sine,
            second_half * cosine + direction * first_half * sine,
            tensor[..., ROT:],
        ],
        axis=-1,
    )


def fetch_forward(gain, shift, matrix, bias, other_matrix, other_bias):
    return (
        lax.all_gather(gain.astype(jnp.bfloat16), "dp", axis=0, tiled=True).astype(gain.dtype),
        lax.all_gather(shift.astype(jnp.bfloat16), "dp", axis=0, tiled=True).astype(shift.dtype),
        lax.all_gather(matrix, "dp", axis=0, tiled=True),
        lax.all_gather(bias.astype(jnp.bfloat16), "dp", axis=0, tiled=True).astype(bias.dtype),
        lax.all_gather(other_matrix, "dp", axis=0, tiled=True),
        lax.all_gather(other_bias.astype(jnp.bfloat16), "dp", axis=0, tiled=True).astype(
            other_bias.dtype
        ),
    )


def fetch_backward(gain, shift, matrix, bias, other_matrix, other_bias):
    return (
        lax.all_gather(gain.astype(jnp.bfloat16), "dp", axis=0, tiled=True).astype(gain.dtype),
        lax.all_gather(shift.astype(jnp.bfloat16), "dp", axis=0, tiled=True).astype(shift.dtype),
        lax.all_gather(matrix, "dp", axis=0, tiled=True),
        lax.all_gather(bias.astype(jnp.bfloat16), "dp", axis=0, tiled=True).astype(bias.dtype),
        lax.all_gather(other_matrix, "dp", axis=0, tiled=True),
        lax.all_gather(other_bias.astype(jnp.bfloat16), "dp", axis=0, tiled=True).astype(
            other_bias.dtype
        ),
    )


def settle(gain_grad, shift_grad, bias_grad, other_bias, left, right, other_left, other_right):
    matrix_grad = jnp.dot(left.T, right, preferred_element_type=jnp.float32)
    other_grad = jnp.dot(other_left.T, other_right, preferred_element_type=jnp.float32)
    shares = (
        lax.psum_scatter(
            gain_grad.astype(jnp.bfloat16), "dp", scatter_dimension=0, tiled=True
        ).astype(jnp.float32),
        lax.psum_scatter(
            shift_grad.astype(jnp.bfloat16), "dp", scatter_dimension=0, tiled=True
        ).astype(jnp.float32),
        lax.psum_scatter(
            matrix_grad.astype(jnp.bfloat16), "dp", scatter_dimension=0, tiled=True
        ).astype(jnp.float32),
        lax.psum_scatter(
            bias_grad.astype(jnp.bfloat16), "dp", scatter_dimension=0, tiled=True
        ).astype(jnp.float32),
        lax.psum_scatter(
            other_grad.astype(jnp.bfloat16), "dp", scatter_dimension=0, tiled=True
        ).astype(jnp.float32),
        lax.psum_scatter(
            other_bias.astype(jnp.bfloat16), "dp", scatter_dimension=0, tiled=True
        ).astype(jnp.float32),
    )
    return (
        lax.psum(shares[0].astype(jnp.bfloat16), "seq").astype(jnp.float32),
        lax.psum(shares[1].astype(jnp.bfloat16), "seq").astype(jnp.float32),
        lax.psum(shares[2].astype(jnp.bfloat16), "seq").astype(jnp.float32),
        lax.psum(shares[3].astype(jnp.bfloat16), "seq").astype(jnp.float32),
        lax.psum(shares[4].astype(jnp.bfloat16), "seq").astype(jnp.float32),
        lax.psum(shares[5].astype(jnp.bfloat16), "seq").astype(jnp.float32),
    )


def block_scores(query_block, key_rows, start):
    scores = jnp.einsum(
        "bqhd,bkhd->bhqk", query_block, key_rows, preferred_element_type=jnp.float32
    ) * HD ** (-0.5)
    length = key_rows.shape[1]
    query_pos = start + jnp.arange(query_block.shape[1], dtype=jnp.int32)
    allowed = jnp.arange(length, dtype=jnp.int32)[None, :] <= query_pos[:, None]
    return jnp.where(allowed[None, None], scores, masked_fill)


def attend(grouped):
    queries = grouped[:, :, 0]
    key_rows = grouped[:, :, 1]
    values = grouped[:, :, 2]
    batch_local, length, local_heads, head_size = queries.shape
    block = min(512, length)
    count = length // block

    def one_block(start):
        query_block = lax.dynamic_slice_in_dim(queries, start, block, 1)
        scores = block_scores(query_block, key_rows, start)
        top = jnp.max(scores, axis=-1, keepdims=True)
        logsum = top[..., 0] + jnp.log(jnp.sum(jnp.exp(scores - top), axis=-1))
        probs = jnp.exp(scores - logsum[..., None]).astype(jnp.bfloat16)
        context = jnp.einsum(
            "bhqk,bkhd->bqhd", probs, values, preferred_element_type=jnp.float32
        ).astype(jnp.bfloat16)
        return (context, logsum)

    starts = jnp.arange(count, dtype=jnp.int32) * block
    contexts, logsums = lax.map(one_block, starts)
    context = jnp.transpose(contexts, (1, 0, 2, 3, 4)).reshape(
        batch_local, length, local_heads, head_size
    )
    logsum = jnp.transpose(logsums, (1, 2, 0, 3)).reshape(batch_local, local_heads, length)
    return (context, logsum)


def attend_back(grouped, context, logsum, incoming):
    queries = grouped[:, :, 0]
    key_rows = grouped[:, :, 1]
    values = grouped[:, :, 2]
    batch_local, length, local_heads, head_size = queries.shape
    block = min(512, length)
    count = length // block
    delta = jnp.sum(incoming.astype(jnp.float32) * context.astype(jnp.float32), axis=-1)

    def one_block(carry, start):
        key_total, value_total = carry
        query_block = lax.dynamic_slice_in_dim(queries, start, block, 1)
        grad_block = lax.dynamic_slice_in_dim(incoming, start, block, 1)
        logsum_block = lax.dynamic_slice_in_dim(logsum, start, block, 2)
        delta_block = jnp.transpose(lax.dynamic_slice_in_dim(delta, start, block, 1), (0, 2, 1))
        scores = block_scores(query_block, key_rows, start)
        probs_f = jnp.exp(scores - logsum_block[..., None])
        probs = probs_f.astype(jnp.bfloat16)
        value_total = value_total + jnp.einsum(
            "bhqk,bqhd->bkhd", probs, grad_block, preferred_element_type=jnp.float32
        )
        prob_grad = jnp.einsum(
            "bqhd,bkhd->bhqk", grad_block, values, preferred_element_type=jnp.float32
        )
        score_grad = (probs_f * (prob_grad - delta_block[..., None]) * HD ** (-0.5)).astype(
            jnp.bfloat16
        )
        query_part = jnp.einsum(
            "bhqk,bkhd->bqhd", score_grad, key_rows, preferred_element_type=jnp.float32
        )
        key_total = key_total + jnp.einsum(
            "bhqk,bqhd->bkhd", score_grad, query_block, preferred_element_type=jnp.float32
        )
        return ((key_total, value_total), query_part)

    empty = jnp.zeros(queries.shape, jnp.float32)
    starts = jnp.arange(count, dtype=jnp.int32) * block
    totals, query_parts = lax.scan(one_block, (empty, empty), starts)
    query_grad = jnp.transpose(query_parts, (1, 0, 2, 3, 4)).reshape(
        batch_local, length, local_heads, head_size
    )
    return jnp.stack([query_grad, totals[0], totals[1]], axis=2).astype(jnp.bfloat16)


def local(
    layer_input,
    cotangent,
    ln1_gain,
    ln1_bias,
    w_qkv,
    b_qkv,
    w_out,
    b_out,
    ln2_gain,
    ln2_bias,
    w_up,
    b_up,
    w_down,
    b_down,
):
    batch_local, tok_local, width = layer_input.shape
    token_count = batch_local * tok_local
    offset = lax.axis_index("seq") * tok_local
    positions = (offset + jnp.arange(tok_local, dtype=jnp.int32)).astype(jnp.float32)
    cosine, sine = angles(positions)
    cosine = cosine[None, :, None, :]
    sine = sine[None, :, None, :]
    gain_one, shift_one, triple_w, triple_b, out_w, out_b = fetch_forward(
        ln1_gain, ln1_bias, w_qkv, b_qkv, w_out, b_out
    )
    rows = layer_input.reshape(token_count, width).astype(jnp.float32)
    normed_one, factor_one, attn_in = normalize(rows, gain_one, shift_one)
    attn_in = attn_in.astype(jnp.bfloat16)
    triple = (jnp.dot(attn_in, triple_w, preferred_element_type=jnp.float32) + triple_b).reshape(
        batch_local, tok_local, 3, H, HD
    )
    queries = rotate(triple[:, :, 0], cosine, sine, 1.0)
    key_rows = rotate(triple[:, :, 1], cosine, sine, 1.0)
    stacked = jnp.stack([queries, key_rows, triple[:, :, 2]], axis=2).astype(jnp.bfloat16)
    grouped = lax.all_to_all(stacked, "seq", split_axis=3, concat_axis=1, tiled=True)
    context, logsum = attend(grouped)
    context_tokens = lax.all_to_all(context, "seq", split_axis=1, concat_axis=2, tiled=True)
    merged = context_tokens.reshape(token_count, width)
    attended = jnp.dot(merged, out_w, preferred_element_type=jnp.float32) + out_b
    gain_two, shift_two, up_w, up_b, down_w, down_b = fetch_forward(
        ln2_gain, ln2_bias, w_up, b_up, w_down, b_down
    )
    normed_two, factor_two, mlp_in = normalize(rows, gain_two, shift_two)
    mlp_in = mlp_in.astype(jnp.bfloat16)
    inner = jnp.dot(mlp_in, up_w, preferred_element_type=jnp.float32) + up_b
    hidden = gelu_value(inner).astype(jnp.bfloat16)
    output = rows + attended + jnp.dot(hidden, down_w, preferred_element_type=jnp.float32) + down_b
    incoming = cotangent.reshape(token_count, width)
    grad_rows = incoming.astype(jnp.float32)
    gain_two, shift_two, up_w, up_b, down_w, down_b = fetch_backward(
        ln2_gain, ln2_bias, w_up, b_up, w_down, b_down
    )
    b_down_grad = jnp.sum(grad_rows, axis=0)
    inner_grad = jnp.dot(incoming, down_w.T, preferred_element_type=jnp.float32) * gelu_slope(inner)
    inner_grad_b = inner_grad.astype(jnp.bfloat16)
    b_up_grad = jnp.sum(inner_grad, axis=0)
    mlp_in_grad = jnp.dot(inner_grad_b, up_w.T, preferred_element_type=jnp.float32)
    ln2_gain_grad = jnp.sum(mlp_in_grad * normed_two, axis=0)
    ln2_bias_grad = jnp.sum(mlp_in_grad, axis=0)
    mlp_grads = settle(
        ln2_gain_grad, ln2_bias_grad, b_up_grad, b_down_grad, mlp_in, inner_grad_b, hidden, incoming
    )
    mlp_back = normalize_back(mlp_in_grad, normed_two, factor_two, gain_two)
    gain_one, shift_one, triple_w, triple_b, out_w, out_b = fetch_backward(
        ln1_gain, ln1_bias, w_qkv, b_qkv, w_out, b_out
    )
    b_out_grad = jnp.sum(grad_rows, axis=0)
    context_grad = (
        jnp.dot(incoming, out_w.T, preferred_element_type=jnp.float32)
        .astype(jnp.bfloat16)
        .reshape(batch_local, tok_local, H, HD)
    )
    grouped_grad = lax.all_to_all(context_grad, "seq", split_axis=2, concat_axis=1, tiled=True)
    triple_heads = attend_back(grouped, context, logsum, grouped_grad)
    token_grad = lax.all_to_all(
        triple_heads, "seq", split_axis=1, concat_axis=3, tiled=True
    ).astype(jnp.float32)
    query_back = rotate(token_grad[:, :, 0], cosine, sine, -1.0)
    key_back = rotate(token_grad[:, :, 1], cosine, sine, -1.0)
    triple_grad = jnp.stack([query_back, key_back, token_grad[:, :, 2]], axis=2).reshape(
        token_count, 3 * width
    )
    triple_grad_b = triple_grad.astype(jnp.bfloat16)
    b_qkv_grad = jnp.sum(triple_grad, axis=0)
    attn_in_grad = jnp.dot(triple_grad_b, triple_w.T, preferred_element_type=jnp.float32)
    ln1_gain_grad = jnp.sum(attn_in_grad * normed_one, axis=0)
    ln1_bias_grad = jnp.sum(attn_in_grad, axis=0)
    attn_grads = settle(
        ln1_gain_grad,
        ln1_bias_grad,
        b_qkv_grad,
        b_out_grad,
        attn_in,
        triple_grad_b,
        merged,
        incoming,
    )
    grad_total = (
        grad_rows + normalize_back(attn_in_grad, normed_one, factor_one, gain_one) + mlp_back
    )
    return (
        output.reshape(layer_input.shape),
        grad_total.reshape(layer_input.shape),
        attn_grads[0],
        attn_grads[1],
        attn_grads[2],
        attn_grads[3],
        attn_grads[4],
        attn_grads[5],
        mlp_grads[0],
        mlp_grads[1],
        mlp_grads[2],
        mlp_grads[3],
        mlp_grads[4],
        mlp_grads[5],
    )


def solution(mesh):
    in_specs = (
        P("dp", "seq", None),
        P("dp", "seq", None),
        P("dp"),
        P("dp"),
        P("dp", None),
        P("dp"),
        P("dp", None),
        P("dp"),
        P("dp"),
        P("dp"),
        P("dp", None),
        P("dp"),
        P("dp", None),
        P("dp"),
    )
    out_specs = (
        P("dp", "seq", None),
        P("dp", "seq", None),
        P("dp"),
        P("dp"),
        P("dp", None),
        P("dp"),
        P("dp", None),
        P("dp"),
        P("dp"),
        P("dp"),
        P("dp", None),
        P("dp"),
        P("dp", None),
        P("dp"),
    )
    return jax.shard_map(local, mesh=mesh, in_specs=in_specs, out_specs=out_specs, check_vma=False)
```

profile of v0, /device:TPU:0, one launch (start us, length us, event | category | flops | bytes accessed | tf_op | source)
XLA Modules:
  0.0 1625.2 jit_solution(7226123091825915187)
XLA Ops:
  10.1 10.6 all-gather.2
  38.8 28.2 %all-gather.14.cloned.1.call-done = bf16[2048,2048]{1,0:T(8,128)(2,1)} async-done(((bf16[256,2048]{1,0:T(8,128)(2,1)}), bf16[2048,2048]{1,0:T(8,128)(2,1)}) %all-gather.14.cloned.1.call-update) | async-done | bytes 8388624 | tf_op jit(solution)/shard_map/all_gather | solution.py:65
  78.8 115.2 %all-gather.12.cloned.1.call-done = bf16[2048,6144]{1,0:T(8,128)(2,1)} async-done(((bf16[256,6144]{1,0:T(8,128)(2,1)}), bf16[2048,6144]{1,0:T(8,128)(2,1)}) %all-gather.12.cloned.1.call-update) | async-done | bytes 25165840 | tf_op jit(solution)/shard_map/all_gather | solution.py:63
  194.0 13.4 convolution_add_fusion.1
  226.8 32.4 %all-to-all-done = bf16[1,128,3,8,256]{1,4,2,0,3:T(8,128)(2,1)S(1)} async-done(((bf16[1,128,3,8,256]{1,4,2,0,3:T(8,128)(2,1)}), bf16[1,128,3,8,256]{1,4,2,0,3:T(8,128)(2,1)S(1)}, u32[]{:S(2)}, u32[]{:S(2)}) %all-to-all-start) | async-done | bytes 1572896 | tf_op jit(solution)/shard_map/all_to_all | solution.py:235
  265.8 16.3 %all_to_all.57 = bf16[1,512,2,256]{3,2,0,1:T(2,128)(2,1)S(1)} all-to-all(bf16[1,512,2,256]{3,2,0,1:T(2,128)(2,1)S(1)} %copy.88), channel_id=1, replica_groups=mesh['dp'=8,'seq'=4] {'seq'}, dimensions={1} | all-to-all | bytes 1048576 | tf_op jit(solution)/shard_map/all_to_all | solution.py:237
  297.3 39.6 %all_to_all.58 = bf16[1,512,3,2,256]{4,3,2,0,1:T(2,128)(2,1)S(1)} all-to-all(bf16[1,512,3,2,256]{4,3,2,0,1:T(2,128)(2,1)} %copy.101), channel_id=1, replica_groups=mesh['dp'=8,'seq'=4] {'seq'}, dimensions={1} | all-to-all | bytes 3145728 | tf_op jit(solution)/shard_map/all_to_all | solution.py:275
  344.2 12.4 convolution_convert_fusion.2
  374.2 9.5 all-gather.4
  383.8 17.2 %convolution_add_fusion = f32[128,8192]{1,0:T(8,128)} fusion(bf16[2048,8192]{1,0:T(8,128)(2,1)} %all-gather.16.cloned.1.call-done, f32[8192]{0:T(1024)S(1)} %convert_element_type.309, bf16[1,128,2048]{2,1,0:T(8,128)(2,1)S(1)} %copy-done.1, f32[2048]{0:T(1024)S(1)} %bitcast.228, f32[2048]{0:T(1024)S(1)} %bitcast.222, f32[128]{0:T(128)S(1)} %add_rsqrt_fusion, ...), kind=kOutput, calls=%fused_computation.4 | convolution fusion | flops 4297588736 | bytes 38323200 | tf_op jit(solution)/shard_map/dot_general | solution.py:245
  401.0 118.0 %all-gather.18.cloned.1.call-done = bf16[8192,2048]{1,0:T(8,128)(2,1)} async-done(((bf16[1024,2048]{1,0:T(8,128)(2,1)}), bf16[8192,2048]{1,0:T(8,128)(2,1)}) %all-gather.18.cloned.1.call-update) | async-done | bytes 33554448 | tf_op jit(solution)/shard_map/all_gather | solution.py:65
  519.1 19.8 %fusion.68 = (bf16[8192]{0:T(1024)(128)(2,1)S(1)}, bf16[128,8192]{1,0:T(8,128)(2,1)}) fusion(f32[128,8192]{1,0:T(8,128)} %convolution_add_fusion, bf16[8192,2048]{1,0:T(8,128)(2,1)} %all-gather.18.cloned.1.call-done, bf16[1,128,2048]{2,1,0:T(8,128)(2,1)S(1)} %copy-done.4), kind=kOutput, calls=%fused_computation.128 | convolution fusion | flops 4306493440 | bytes 40386560 | tf_op jit(solution)/shard_map/dot_general | solution.py:254
  538.9 16.0 convolution_convert_fusion
  555.3 16.3 %convolution_convert_fusion.1 = bf16[8192,2048]{1,0:T(8,128)(2,1)} fusion(bf16[1,128,2048]{2,1,0:T(8,128)(2,1)S(1)} %copy-done.4, f32[128,8192]{1,0:T(8,128)} %convolution_add_fusion), kind=kOutput, calls=%fused_computation.1 | convolution fusion | flops 4316987392 | bytes 38273024 | tf_op jit(solution)/shard_map/dot_general | solution.py:87
  571.7 22.8 %reduce-scatter.7.cloned.1.call-done = bf16[256,2048]{1,0:T(8,128)(2,1)} async-done(((bf16[2048,2048]{1,0:T(8,128)(2,1)}), bf16[256,2048]{1,0:T(8,128)(2,1)}) %reduce-scatter.7.cloned.1.call-update) | async-done | bytes 1048592 | tf_op jit(solution)/shard_map/reduce_scatter | solution.py:101
  594.5 159.8 %reduce-scatter.5.cloned.1.call-done = bf16[256,6144]{1,0:T(8,128)(2,1)} async-done(((bf16[2048,6144]{1,0:T(8,128)(2,1)}), bf16[256,6144]{1,0:T(8,128)(2,1)}) %reduce-scatter.5.cloned.1.call-update) | async-done | bytes 3145744 | tf_op jit(solution)/shard_map/reduce_scatter | solution.py:95
  754.3 209.1 %reduce-scatter.9.cloned.1.call-done = bf16[256,8192]{1,0:T(8,128)(2,1)} async-done(((bf16[2048,8192]{1,0:T(8,128)(2,1)}), bf16[256,8192]{1,0:T(8,128)(2,1)}) %reduce-scatter.9.cloned.1.call-update) | async-done | bytes 4194320 | tf_op jit(solution)/shard_map/reduce_scatter | solution.py:95
  963.4 209.1 %reduce-scatter.11.cloned.1.call-done = bf16[1024,2048]{1,0:T(8,128)(2,1)} async-done(((bf16[8192,2048]{1,0:T(8,128)(2,1)}), bf16[1024,2048]{1,0:T(8,128)(2,1)}) %reduce-scatter.11.cloned.1.call-update) | async-done | bytes 4194320 | tf_op jit(solution)/shard_map/reduce_scatter | solution.py:101
  1200.4 17.1 %fusion.46 = f32[128,2048]{1,0:T(8,128)} fusion(bf16[2048,8192]{1,0:T(8,128)(2,1)} %all-gather.16.cloned.1.call-done, bf16[128,8192]{1,0:T(8,128)(2,1)S(1)} %copy-done.5), kind=kOutput, calls=%fused_computation.80 | convolution fusion | flops 4294967296 | bytes 36700160 | tf_op jit(solution)/shard_map/dot_general | solution.py:257
  1217.5 14.5 fusion.38
  1232.0 25.7 %all-reduce.7 = (bf16[2048]{0:T(1024)(128)(2,1)S(1)}, bf16[2048]{0:T(1024)(128)(2,1)S(1)}, bf16[6144]{0:T(1024)(128)(2,1)S(1)}, bf16[2048]{0:T(1024)(128)(2,1)S(...) all-reduce(bf16[2048]{0:T(1024)(128)(2,1)S(1)} %get-tuple-element.6, ...), channel_id=2, replica_groups=mesh['dp'=8,'seq'=4] {'dp'}, use_global_device_ids=true, to_apply=%region_10.11.clone | all-reduce | flops 24576 | bytes 98304
  1258.2 14.3 all-reduce.8
  1279.3 14.6 fusion.5
  1293.9 308.1 %all-reduce.12.cloned.1.call-done = (bf16[256,6144]{1,0:T(8,128)(2,1)}, bf16[256,2048]{1,0:T(8,128)(2,1)}, bf16[256,8192]{1,0:T(8,128)(2,1)}, bf16[1024,2048]{1,0:T(8,128)(2,1)}) async-done(((bf16[256,6144]{1,0:T(8,128)(2,1)}, bf16[256,2048]{1,0:T(8,128)(2,1)}, bf16[256,8192]{1,0:T(8,128)(2,1)}, bf16[1024,2048]{1,0:T(8,128)(2,1)}), (bf16[256,6144]{1,0:T(8,128)(2,1)}, bf16[256,2048]{1,0:T(8,128)(2,1)}, ...) | async-done | bytes 12582928 | tf_op jit(solution)/shard_map/psum | solution.py:111
  (184 shorter events, 148.6 us)
Async XLA Ops:
  7.2 59.8 %all-gather.14.cloned.1.call-start = ((), (), s32[]{:S(2)}) async-start(), calls=%async_computation.9 | async-start | bytes 9437184 | tf_op jit(solution)/shard_map/all_gather | solution.py:65
  7.9 186.1 %all-gather.12.cloned.1.call-start = ((), (), s32[]{:S(2)}) async-start(), calls=%async_computation.8 | async-start | bytes 28311552 | tf_op jit(solution)/shard_map/all_gather | solution.py:63
  8.7 375.2 %all-gather.16.cloned.1.call-start = ((), (), s32[]{:S(2)}) async-start(), calls=%async_computation.10 | async-start | bytes 37748736 | tf_op jit(solution)/shard_map/all_gather | solution.py:63
  9.4 11.3 copy-start.22
  9.4 20.5 %copy-start.23 = (f32[256]{0:T(256)S(1)}, f32[256]{0:T(256)}, u32[]{:S(2)}) copy-start(f32[256]{0:T(256)} %param.16) | copy-start | bytes 3076
  9.4 28.7 %copy-start.1 = (bf16[1,128,2048]{2,1,0:T(8,128)(2,1)S(1)}, bf16[1,128,2048]{2,1,0:T(8,128)(2,1)}, u32[]{:S(2)}) copy-start(bf16[1,128,2048]{2,1,0:T(8,128)(2,1)} %param.14) | copy-start | bytes 1572868
  9.4 57.5 %copy-start.4 = (bf16[1,128,2048]{2,1,0:T(8,128)(2,1)S(1)}, bf16[1,128,2048]{2,1,0:T(8,128)(2,1)}, u32[]{:S(2)}) copy-start(bf16[1,128,2048]{2,1,0:T(8,128)(2,1)} %param.15) | copy-start | bytes 1572868
  9.4 509.6 %all-gather.18.cloned.1.call-start = ((), (), s32[]{:S(2)}) async-start(), calls=%async_computation.11 | async-start | bytes 37748736 | tf_op jit(solution)/shard_map/all_gather | solution.py:65
  74.2 142.1 %all-to-all-start.2 = ((bf16[1,128,8,256]{3,1,0,2:T(8,128)(2,1)}), bf16[1,128,8,256]{3,1,0,2:T(8,128)(2,1)S(1)}, u32[]{:S(2)}, u32[]{:S(2)}) async-start(bf16[1,128,8,256]{3,1,0,2:T(8,128)(2,1)} %copy.91), calls=%async_computation.2 | async-start | bytes 1048576 | tf_op jit(solution)/shard_map/all_to_all | solution.py:273
  217.1 42.1 %all-to-all-start = ((bf16[1,128,3,8,256]{1,4,2,0,3:T(8,128)(2,1)}), bf16[1,128,3,8,256]{1,4,2,0,3:T(8,128)(2,1)S(1)}, u32[]{:S(2)}, u32[]{:S(2)}) async-start(bf16[1,128,3,8,256]{1,4,2,0,3:T(8,128)(2,1)} %copy.84), calls=%async_computation | async-start | bytes 3145728 | tf_op jit(solution)/shard_map/all_to_all | solution.py:235
  221.9 372.6 %reduce-scatter.7.cloned.1.call-start = ((), (), s32[]{:S(2)}) async-start(), calls=%async_computation.13 | async-start | bytes 9437184 | tf_op jit(solution)/shard_map/reduce_scatter | solution.py:101
  288.3 466.0 %reduce-scatter.5.cloned.1.call-start = ((), (), s32[]{:S(2)}) async-start(), calls=%async_computation.12 | async-start | bytes 28311552 | tf_op jit(solution)/shard_map/reduce_scatter | solution.py:95
  356.6 9.6 copy-start.24
  356.6 17.6 %copy-start.25 = (f32[256]{0:T(256)S(1)}, f32[256]{0:T(256)}, u32[]{:S(2)}) copy-start(f32[256]{0:T(256)} %param.22) | copy-start | bytes 3076
  356.6 606.7 %reduce-scatter.9.cloned.1.call-start = ((), (), s32[]{:S(2)}) async-start(), calls=%async_computation.14 | async-start | bytes 37748736 | tf_op jit(solution)/shard_map/reduce_scatter | solution.py:95
  554.9 617.6 %reduce-scatter.11.cloned.1.call-start = ((), (), s32[]{:S(2)}) async-start(), calls=%async_computation.15 | async-start | bytes 37748736 | tf_op jit(solution)/shard_map/reduce_scatter | solution.py:101
  571.6 1030.4 %all-reduce.12.cloned.1.call-start = ((), (), s32[]{:S(2)}) async-start(), calls=%async_computation.16 | async-start | bytes 25165824 | tf_op jit(solution)/shard_map/psum | solution.py:111
  1172.4 9.6 copy-start.27
  1172.4 17.7 %copy-start.28 = (u32[32]{0:T(128)S(1)}, u32[32]{0:T(128)}, u32[]{:S(2)}) copy-start(u32[32]{0:T(128)} %constant.88) | copy-start | bytes 388
  1192.7 6.1 copy-start.8
  1192.7 6.1 copy-start.10
  1272.5 6.8 copy-start
  1274.2 343.7 %copy-start.21 = (f32[256]{0:T(256)}, f32[256]{0:T(256)S(1)}, u32[]{:S(2)}) copy-start(f32[256]{0:T(256)S(1)} %convert_element_type.339) | copy-start | bytes 3076
  1602.0 7.1 copy-start.16
  (16 other events, 37.9 us)
Sparse Core Ops, SparseCore 0:
  9.9 57.0 all-gather.13
  68.8 125.1 all-gather.11
  195.9 160.6 all-gather.15
  358.4 160.6 all-gather.17
  523.0 71.4 reduce-scatter.6
  598.0 156.2 reduce-scatter.4
  757.9 205.4 reduce-scatter.8
  966.9 205.4 reduce-scatter.10
  1175.3 426.6 all-reduce.11
where the time goes:
time: 1630 us
  waiting for transfers between devices  1210 us (74%)
  blocking collectives  167 us (10%)
  matrix products  167 us (10%)
  local copies, waits for them, and re-layouts  32.8 us (2%)
  other arithmetic  25.8 us (2%)
  between operations  16.6 us (1%)
    reduce_scatter x2, waiting for transfers between devices, settle(): lax.psum_scatter(matrix_grad.astype(jnp.bfloat16), 'dp', scatter_dimensio...  369 us
    psum x1, waiting for transfers between devices, settle(): lax.psum(shares[2].astype(jnp.bfloat16), 'seq').astype(jnp.float32)  308 us
    reduce_scatter x2, waiting for transfers between devices, settle(): lax.psum_scatter(other_grad.astype(jnp.bfloat16), 'dp', scatter_dimension...  232 us
    all_gather x2, waiting for transfers between devices, fetch_forward(): lax.all_gather(other_matrix, 'dp', axis=0, tiled=True)  146 us
    all_gather x2, waiting for transfers between devices, fetch_forward(): lax.all_gather(matrix, 'dp', axis=0, tiled=True)  115 us
    all_to_all x1, blocking collectives, local(): lax.all_to_all(triple_heads, 'seq', split_axis=1, concat_axis=3, tiled=True)  39.6 us
  transfers between devices with their start and end apart: 11, of which 9 were waited for; matrix products, arithmetic and copies ran while one was open for 13% of the time, Pallas kernels for 0%

commit v1 on v0

--- a/solution.py
+++ b/solution.py
@@ -108,7 +108,7 @@
     return (
         lax.psum(shares[0].astype(jnp.bfloat16), "seq").astype(jnp.float32),
         lax.psum(shares[1].astype(jnp.bfloat16), "seq").astype(jnp.float32),
-        lax.psum(shares[2].astype(jnp.bfloat16), "seq").astype(jnp.float32),
+        jnp.sum(lax.all_gather(shares[2].astype(jnp.bfloat16), "seq"), axis=0).astype(jnp.float32),
         lax.psum(shares[3].astype(jnp.bfloat16), "seq").astype(jnp.float32),
         lax.psum(shares[4].astype(jnp.bfloat16), "seq").astype(jnp.float32),
         lax.psum(shares[5].astype(jnp.bfloat16), "seq").astype(jnp.float32),

time: 1630 us -> 1900 us (1.17)
  waiting for transfers between devices: 1210 us -> 1440 us
  other arithmetic: 25.8 us -> 49.3 us
    all_gather x0 -> x2, waiting for transfers between devices: none -> 372 us  [settle(): lax.all_gather(shares[2].astype(jnp.bfloat16), 'seq')]
    psum x1, waiting for transfers between devices: 308 us -> 179 us  [settle(): lax.psum(shares[4].astype(jnp.bfloat16), 'seq').astype(jnp.float32)]
    reduce_scatter x2, waiting for transfers between devices: 232 us -> 284 us  [settle(): lax.psum_scatter(other_grad.astype(jnp.bfloat16), 'dp', scatter_dimension...]
    reduce_scatter x2, waiting for transfers between devices: 369 us -> 328 us  [settle(): lax.psum_scatter(matrix_grad.astype(jnp.bfloat16), 'dp', scatter_dimensio...]
  transfers between devices with their start and end apart: 11 -> 13, of which waited for: 9 -> 11; matrix products, arithmetic and copies ran while one was open for 13% -> 12% of each run, Pallas kernels for 0% -> 0%
where the time goes in v1:
time: 1900 us
  waiting for transfers between devices  1440 us (76%)
  blocking collectives  173 us (9%)
  matrix products  164 us (9%)
  other arithmetic  49.3 us (3%)
  local copies, waits for them, and re-layouts  38.6 us (2%)
    all_gather x2, waiting for transfers between devices, settle(): lax.all_gather(shares[2].astype(jnp.bfloat16), 'seq')  372 us
    reduce_scatter x2, waiting for transfers between devices, settle(): lax.psum_scatter(matrix_grad.astype(jnp.bfloat16), 'dp', scatter_dimensio...  328 us
    reduce_scatter x2, waiting for transfers between devices, settle(): lax.psum_scatter(other_grad.astype(jnp.bfloat16), 'dp', scatter_dimension...  284 us
    psum x1, waiting for transfers between devices, settle(): lax.psum(shares[4].astype(jnp.bfloat16), 'seq').astype(jnp.float32)  179 us
    all_gather x2, waiting for transfers between devices, fetch_forward(): lax.all_gather(other_matrix, 'dp', axis=0, tiled=True)  132 us
    all_gather x2, waiting for transfers between devices, fetch_forward(): lax.all_gather(matrix, 'dp', axis=0, tiled=True)  115 us
    all_to_all x1, blocking collectives, local(): lax.all_to_all(triple_heads, 'seq', split_axis=1, concat_axis=3, tiled=True)  39.4 us
  transfers between devices with their start and end apart: 13, of which 11 were waited for; matrix products, arithmetic and copies ran while one was open for 12% of the time, Pallas kernels for 0%

profile of v1, /device:TPU:0, one launch (start us, length us, event | category | flops | bytes accessed | tf_op | source)
XLA Modules:
  0.0 1895.1 jit_solution(16420096054747878034)
XLA Ops:
  38.8 28.2 %all-gather.18.cloned.1.call-done = bf16[2048,2048]{1,0:T(8,128)(2,1)} async-done(((bf16[256,2048]{1,0:T(8,128)(2,1)}), bf16[2048,2048]{1,0:T(8,128)(2,1)}) %all-gather.18.cloned.1.call-update) | async-done | bytes 8388624 | tf_op jit(solution)/shard_map/all_gather | solution.py:65
  78.8 115.2 %all-gather.16.cloned.1.call-done = bf16[2048,6144]{1,0:T(8,128)(2,1)} async-done(((bf16[256,6144]{1,0:T(8,128)(2,1)}), bf16[2048,6144]{1,0:T(8,128)(2,1)}) %all-gather.16.cloned.1.call-update) | async-done | bytes 25165840 | tf_op jit(solution)/shard_map/all_gather | solution.py:63
  194.0 13.4 convolution_add_fusion.1
  228.8 30.4 %all-to-all-done = bf16[1,128,3,8,256]{1,4,2,0,3:T(8,128)(2,1)S(1)} async-done(((bf16[1,128,3,8,256]{1,4,2,0,3:T(8,128)(2,1)}), bf16[1,128,3,8,256]{1,4,2,0,3:T(8,128)(2,1)S(1)}, u32[]{:S(2)}, u32[]{:S(2)}) %all-to-all-start) | async-done | bytes 1572896 | tf_op jit(solution)/shard_map/all_to_all | solution.py:235
  270.6 39.4 %all_to_all.57 = bf16[1,512,3,2,256]{4,3,2,0,1:T(2,128)(2,1)S(1)} all-to-all(bf16[1,512,3,2,256]{4,3,2,0,1:T(2,128)(2,1)} %copy.101), channel_id=1, replica_groups=mesh['dp'=8,'seq'=4] {'seq'}, dimensions={1} | all-to-all | bytes 3145728 | tf_op jit(solution)/shard_map/all_to_all | solution.py:275
  317.2 12.0 convolution_convert_fusion.2
  331.3 17.2 all_to_all.58
  385.0 13.1 convolution_add_fusion
  400.0 14.8 convolution_convert_fusion.1
  415.2 103.9 %all-gather.22.cloned.1.call-done = bf16[8192,2048]{1,0:T(8,128)(2,1)} async-done(((bf16[1024,2048]{1,0:T(8,128)(2,1)}), bf16[8192,2048]{1,0:T(8,128)(2,1)}) %all-gather.22.cloned.1.call-update) | async-done | bytes 33554448 | tf_op jit(solution)/shard_map/all_gather | solution.py:65
  519.1 19.8 %fusion.68 = (bf16[8192]{0:T(1024)(128)(2,1)S(1)}, bf16[128,8192]{1,0:T(8,128)(2,1)}) fusion(f32[128,8192]{1,0:T(8,128)} %copy-done, bf16[8192,2048]{1,0:T(8,128)(2,1)} %all-gather.22.cloned.1.call-done, bf16[1,128,2048]{2,1,0:T(8,128)(2,1)S(1)} %copy-done.4), kind=kOutput, calls=%fused_computation.128 | convolution fusion | flops 4306493440 | bytes 40386560 | tf_op jit(solution)/shard_map/dot_general | solution.py:254
  538.9 20.8 %convolution_convert_fusion = bf16[2048,8192]{1,0:T(8,128)(2,1)} fusion(bf16[128,8192]{1,0:T(8,128)(2,1)} %get-tuple-element.116, bf16[1,128,2048]{2,1,0:T(8,128)(2,1)S(1)} %copy-done.2, f32[2048]{0:T(1024)S(1)} %bitcast.233, f32[2048]{0:T(1024)S(1)} %bitcast.227, f32[128]{0:T(128)S(1)} %add_rsqrt_fusion, f32[128]{0:T(128)S(1)} %broadcast_multiply_fusion.5), kind=kOutput, calls=%fused_computation | convolution fusion | flops 4313317376 | bytes 36193280 | tf_op jit(solution)/shard_map/dot_general | solution.py:86
  559.8 119.1 %reduce-scatter.5.cloned.1.call-done = bf16[256,6144]{1,0:T(8,128)(2,1)} async-done(((bf16[2048,6144]{1,0:T(8,128)(2,1)}), bf16[256,6144]{1,0:T(8,128)(2,1)}) %reduce-scatter.5.cloned.1.call-update) | async-done | bytes 3145744 | tf_op jit(solution)/shard_map/reduce_scatter | solution.py:95
  678.9 75.3 %reduce-scatter.7.cloned.1.call-done = bf16[256,2048]{1,0:T(8,128)(2,1)} async-done(((bf16[2048,2048]{1,0:T(8,128)(2,1)}), bf16[256,2048]{1,0:T(8,128)(2,1)}) %reduce-scatter.7.cloned.1.call-update) | async-done | bytes 1048592 | tf_op jit(solution)/shard_map/reduce_scatter | solution.py:101
  754.3 209.1 %reduce-scatter.11.cloned.1.call-done = bf16[1024,2048]{1,0:T(8,128)(2,1)} async-done(((bf16[8192,2048]{1,0:T(8,128)(2,1)}), bf16[1024,2048]{1,0:T(8,128)(2,1)}) %reduce-scatter.11.cloned.1.call-update) | async-done | bytes 4194320 | tf_op jit(solution)/shard_map/reduce_scatter | solution.py:101
  963.5 209.0 %reduce-scatter.9.cloned.1.call-done = bf16[256,8192]{1,0:T(8,128)(2,1)} async-done(((bf16[2048,8192]{1,0:T(8,128)(2,1)}), bf16[256,8192]{1,0:T(8,128)(2,1)}) %reduce-scatter.9.cloned.1.call-update) | async-done | bytes 4194320 | tf_op jit(solution)/shard_map/reduce_scatter | solution.py:95
  1200.2 16.9 fusion.46
  1217.1 14.5 fusion.38
  1231.6 25.7 %all-reduce.7 = (bf16[2048]{0:T(1024)(128)(2,1)S(1)}, bf16[2048]{0:T(1024)(128)(2,1)S(1)}, bf16[6144]{0:T(1024)(128)(2,1)S(1)}, bf16[2048]{0:T(1024)(128)(2,1)S(...) all-reduce(bf16[2048]{0:T(1024)(128)(2,1)S(1)} %get-tuple-element.6, ...), channel_id=4, replica_groups=mesh['dp'=8,'seq'=4] {'dp'}, use_global_device_ids=true, to_apply=%region_10.11.clone | all-reduce | flops 24576 | bytes 98304
  1257.8 19.0 %all-reduce.8 = (bf16[256]{0:T(256)(128)(2,1)S(1)}, bf16[256]{0:T(256)(128)(2,1)S(1)}, bf16[768]{0:T(1024)(128)(2,1)S(1)}, bf16[256]{0:T(256)(128)(2,1)S(1)}, bf...) all-reduce(bf16[256]{0:T(256)(128)(2,1)S(1)} %dynamic-slice.1, ...), channel_id=1, replica_groups=mesh['dp'=8,'seq'=4] {'seq'}, use_global_device_ids=true, to_apply=%region_11.12 | all-reduce | flops 3072 | bytes 12288 | tf_op jit(solution)/shard_map/psum | solution.py:109
  1283.6 14.1 fusion.5
  1297.8 95.0 %all-gather.24.cloned.1.call-done = bf16[1024,6144]{1,0:T(8,128)(2,1)} async-done(((bf16[256,6144]{1,0:T(8,128)(2,1)}), bf16[1024,6144]{1,0:T(8,128)(2,1)}) %all-gather.24.cloned.1.call-update) | async-done | bytes 12582928 | tf_op jit(solution)/shard_map/all_gather | solution.py:111
  1403.4 178.8 %all-reduce.12.cloned.1.call-done = (bf16[256,2048]{1,0:T(8,128)(2,1)}, bf16[1024,2048]{1,0:T(8,128)(2,1)}) async-done(((bf16[256,2048]{1,0:T(8,128)(2,1)}, bf16[1024,2048]{1,0:T(8,128)(2,1)}), (bf16[256,2048]{1,0:T(8,128)(2,1)}, bf16[1024,2048]{1,0:T(8,128)(2,1)})) %all-reduce.12.cloned.1.call-update) | async-done | bytes 5242896 | tf_op jit(solution)/shard_map/psum | solution.py:113
  1592.5 277.0 %all-gather.26.cloned.1.call-done = bf16[1024,8192]{1,0:T(8,128)(2,1)} async-done(((bf16[256,8192]{1,0:T(8,128)(2,1)}), bf16[1024,8192]{1,0:T(8,128)(2,1)}) %all-gather.26.cloned.1.call-update) | async-done | bytes 16777232 | tf_op jit(solution)/shard_map/all_gather | solution.py:111
  (186 shorter events, 196.8 us)
Async XLA Ops:
  7.2 59.8 %all-gather.18.cloned.1.call-start = ((), (), s32[]{:S(2)}) async-start(), calls=%async_computation.9 | async-start | bytes 9437184 | tf_op jit(solution)/shard_map/all_gather | solution.py:65
  7.9 186.1 %all-gather.16.cloned.1.call-start = ((), (), s32[]{:S(2)}) async-start(), calls=%async_computation.8 | async-start | bytes 28311552 | tf_op jit(solution)/shard_map/all_gather | solution.py:63
  8.7 376.3 %all-gather.20.cloned.1.call-start = ((), (), s32[]{:S(2)}) async-start(), calls=%async_computation.10 | async-start | bytes 37748736 | tf_op jit(solution)/shard_map/all_gather | solution.py:63
  9.4 11.3 copy-start.19
  9.4 20.5 %copy-start.20 = (f32[256]{0:T(256)S(1)}, f32[256]{0:T(256)}, u32[]{:S(2)}) copy-start(f32[256]{0:T(256)} %param.16) | copy-start | bytes 3076
  9.4 28.7 %copy-start.2 = (bf16[1,128,2048]{2,1,0:T(8,128)(2,1)S(1)}, bf16[1,128,2048]{2,1,0:T(8,128)(2,1)}, u32[]{:S(2)}) copy-start(bf16[1,128,2048]{2,1,0:T(8,128)(2,1)} %param.14) | copy-start | bytes 1572868
  9.4 57.5 %copy-start.3 = (bf16[1,128,2048]{2,1,0:T(8,128)(2,1)S(1)}, bf16[1,128,2048]{2,1,0:T(8,128)(2,1)}, u32[]{:S(2)}) copy-start(bf16[1,128,2048]{2,1,0:T(8,128)(2,1)} %param.15) | copy-start | bytes 1572868
  9.4 509.6 %all-gather.22.cloned.1.call-start = ((), (), s32[]{:S(2)}) async-start(), calls=%async_computation.11 | async-start | bytes 37748736 | tf_op jit(solution)/shard_map/all_gather | solution.py:65
  74.2 142.1 %all-to-all-start.2 = ((bf16[1,128,8,256]{3,1,0,2:T(8,128)(2,1)}), bf16[1,128,8,256]{3,1,0,2:T(8,128)(2,1)S(1)}, u32[]{:S(2)}, u32[]{:S(2)}) async-start(bf16[1,128,8,256]{3,1,0,2:T(8,128)(2,1)} %copy.91), calls=%async_computation.2 | async-start | bytes 1048576 | tf_op jit(solution)/shard_map/all_to_all | solution.py:273
  217.1 42.1 %all-to-all-start = ((bf16[1,128,3,8,256]{1,4,2,0,3:T(8,128)(2,1)}), bf16[1,128,3,8,256]{1,4,2,0,3:T(8,128)(2,1)S(1)}, u32[]{:S(2)}, u32[]{:S(2)}) async-start(bf16[1,128,3,8,256]{1,4,2,0,3:T(8,128)(2,1)} %copy.84), calls=%async_computation | async-start | bytes 3145728 | tf_op jit(solution)/shard_map/all_to_all | solution.py:235
  221.9 457.0 %reduce-scatter.5.cloned.1.call-start = ((), (), s32[]{:S(2)}) async-start(), calls=%async_computation.12 | async-start | bytes 28311552 | tf_op jit(solution)/shard_map/reduce_scatter | solution.py:95
  329.3 425.0 %reduce-scatter.7.cloned.1.call-start = ((), (), s32[]{:S(2)}) async-start(), calls=%async_computation.13 | async-start | bytes 9437184 | tf_op jit(solution)/shard_map/reduce_scatter | solution.py:101
  358.2 9.3 copy-start.21
  358.2 17.7 copy-start.22
  358.2 605.1 %reduce-scatter.11.cloned.1.call-start = ((), (), s32[]{:S(2)}) async-start(), calls=%async_computation.15 | async-start | bytes 37748736 | tf_op jit(solution)/shard_map/reduce_scatter | solution.py:101
  414.9 104.2 %copy-start.4 = (bf16[1,128,2048]{2,1,0:T(8,128)(2,1)S(1)}, bf16[1,128,2048]{2,1,0:T(8,128)(2,1)}, u32[]{:S(2)}) copy-start(bf16[1,128,2048]{2,1,0:T(8,128)(2,1)} %param.15) | copy-start | bytes 1572868
  414.9 757.6 %reduce-scatter.9.cloned.1.call-start = ((), (), s32[]{:S(2)}) async-start(), calls=%async_computation.14 | async-start | bytes 37748736 | tf_op jit(solution)/shard_map/reduce_scatter | solution.py:95
  559.7 833.0 %all-gather.24.cloned.1.call-start = ((), (), s32[]{:S(2)}) async-start(), calls=%async_computation.16 | async-start | bytes 15728640 | tf_op jit(solution)/shard_map/all_gather | solution.py:111
  678.9 903.3 %all-reduce.12.cloned.1.call-start = ((), (), s32[]{:S(2)}) async-start(), calls=%async_computation.18 | async-start | bytes 10485760 | tf_op jit(solution)/shard_map/psum | solution.py:113
  963.4 209.1 %copy-start.23 = (f32[256]{0:T(256)S(1)}, f32[256]{0:T(256)}, u32[]{:S(2)}) copy-start(f32[256]{0:T(256)} %param.21) | copy-start | bytes 3076
  963.4 218.0 %copy-start.24 = (f32[256]{0:T(256)S(1)}, f32[256]{0:T(256)}, u32[]{:S(2)}) copy-start(f32[256]{0:T(256)} %param.27) | copy-start | bytes 3076
  963.4 226.6 %copy-start.25 = (u32[32]{0:T(128)S(1)}, u32[32]{0:T(128)}, u32[]{:S(2)}) copy-start(u32[32]{0:T(128)} %constant.90) | copy-start | bytes 388
  963.4 906.1 %all-gather.26.cloned.1.call-start = ((), (), s32[]{:S(2)}) async-start(), calls=%async_computation.17 | async-start | bytes 20971520 | tf_op jit(solution)/shard_map/all_gather | solution.py:111
  1278.6 609.2 %copy-start.18 = (f32[256]{0:T(256)}, f32[256]{0:T(256)S(1)}, u32[]{:S(2)}) copy-start(f32[256]{0:T(256)S(1)} %convert_element_type.343) | copy-start | bytes 3076
  (15 other events, 42.1 us)
Sparse Core Ops, SparseCore 0:
  9.9 57.0 all-gather.17
  68.8 125.1 all-gather.15
  195.9 160.6 all-gather.19
  358.4 160.6 all-gather.21
  522.6 156.2 reduce-scatter.4
  682.8 71.4 reduce-scatter.6
  757.9 205.4 reduce-scatter.10
  966.9 205.4 reduce-scatter.8
  1174.0 218.6 all-gather.23
  1395.0 187.1 all-reduce.11
  1583.8 285.6 all-gather.25
